TPU v7x, 32 devices: a whole 2x2x4 slice. The times are simulated.
32 devices in a mesh: groups: 2 (over y), tensor: 4 (over z), dp: 2 (over x), kv: 2 (over core).
Axes of the slice: x: 2, y: 2, z: 4, core: 2. Of those that a mesh axis runs over, the one named last changes fastest.
Arguments:
- residual: bfloat16 [64, 16384], P(('groups', 'dp'), ('tensor', 'kv')), parts along dimension 0, may hold values from -10 to 10
- query: bfloat16 [64, 8192], P(('groups', 'dp'), ('tensor', 'kv')), parts along dimension 0, may hold values from -60 to 60
- new_pair: bfloat16 [2, 64, 4, 128], P(None, ('groups', 'dp')), parts along dimension 1, may hold values from -8 to 8
- kv_cache: bfloat16 [2, 64, 2048, 4, 128], P(None, ('groups', 'dp'), ('tensor', 'kv')), parts along dimension 1, may hold values from -4.5 to 4.5
- lengths: int32 [64], P(('groups', 'dp')), parts along dimension 0, may hold values from 2 to 2048
- out_weight: bfloat16 [8192, 16384], P(('tensor', 'kv')), may hold values from -0.09375 to 0.09375
- norm_gain: bfloat16 [16384], replicated, may hold values from 0.25 to 1.75
Outputs:
- residual_out: bfloat16 [64, 16384], P(('groups', 'dp'), ('tensor', 'kv')), parts along dimension 0
- mlp_input: bfloat16 [64, 16384], P(('groups', 'dp')), parts along dimension 0
There are 2 independent parts, one for each index of `groups`. A program takes and returns all parts, laid end to end along the dimension named above; an argument that names none is the same for every part. Nothing has to cross between parts.
Inputs may be any that keep to these rules, and one draw needn't show every extreme that they name: Positions below lengths[b] hold sequence b's cache; the others are ignored.
All inputs are finite; a program needn't handle non-finite values.
Results may differ from a plain program's by a relative error of at most 0.007.
Values may be sent and summed in bfloat16 or wider, within the bound.
A program may use at most 128 MiB of HBM per device.

v0:
```python
import math

import jax
import jax.numpy as jnp
from jax import lax
from jax.sharding import PartitionSpec as P

D = 16384
QH = 64
KVH = 4
HD = 128


floor_value = -1e30
epsilon = 1e-05


def on_device(residual, query, new_pair, kv_cache, lengths, out_weight, norm_gain):
    seqs = residual.shape[0]
    width = residual.shape[1]
    per_dev = query.shape[1] // HD
    group = QH // KVH
    scaling = 1.0 / math.sqrt(HD)
    mine = lax.axis_index(("tensor", "kv"))
    queries = lax.all_gather(query, ("tensor", "kv"), axis=1, tiled=True)
    grouped = queries.reshape(seqs, KVH, group, HD)
    span = kv_cache.shape[2]
    places = mine * span + jnp.arange(span, dtype=jnp.int32)
    live = (places[None, :] < lengths[:, None])[:, None, None, :]
    scores = (
        jnp.einsum("bgjd,bpgd->bgjp", grouped, kv_cache[0], preferred_element_type=jnp.float32)
        * scaling
    )
    scores = jnp.where(live, scores, floor_value)
    highest = jnp.max(scores, axis=3)
    weights = jnp.where(live, jnp.exp(scores - highest[..., None]), 0.0)
    totals = jnp.sum(weights, axis=3)
    accum = jnp.einsum("bgjp,bpgd->bgjd", weights, kv_cache[1], preferred_element_type=jnp.float32)
    highest = highest.reshape(seqs, QH)
    totals = totals.reshape(seqs, QH)
    accum = accum.reshape(seqs, QH, HD)
    arrived = (
        lax.all_to_all(highest[None], ("tensor", "kv"), split_axis=2, concat_axis=0, tiled=True),
        lax.all_to_all(totals[None], ("tensor", "kv"), split_axis=2, concat_axis=0, tiled=True),
        lax.all_to_all(accum[None], ("tensor", "kv"), split_axis=2, concat_axis=0, tiled=True),
    )
    best = jnp.max(arrived[0], axis=0)
    factor = jnp.exp(arrived[0] - best[None])
    totals = jnp.sum(arrived[1] * factor, axis=0)
    accum = jnp.sum(arrived[2] * factor[..., None], axis=0)
    highest = best
    own_query = query.reshape(seqs, per_dev, HD).astype(jnp.float32)
    head_ids = mine * per_dev + jnp.arange(per_dev, dtype=jnp.int32)
    selector = (head_ids[:, None] // group == jnp.arange(KVH, dtype=jnp.int32)[None, :]).astype(
        jnp.float32
    )
    fresh_pair = jnp.einsum("hg,sbgd->sbhd", selector, new_pair.astype(jnp.float32))
    fresh = jnp.sum(own_query * fresh_pair[0], axis=2) * scaling
    best = jnp.maximum(highest, fresh)
    old_factor = jnp.exp(highest - best)
    new_factor = jnp.exp(fresh - best)
    totals = totals * old_factor + new_factor
    accum = accum * old_factor[..., None] + new_factor[..., None] * fresh_pair[1]
    attended = (accum / totals[..., None]).astype(jnp.bfloat16).reshape(seqs, per_dev * HD)
    partial_value = jnp.dot(attended, out_weight, preferred_element_type=jnp.float32)
    gain_wide = norm_gain.astype(jnp.float32)
    share = lax.psum_scatter(partial_value, ("tensor", "kv"), scatter_dimension=1, tiled=True)
    stream = (residual.astype(jnp.float32) + share).astype(jnp.bfloat16)
    widened = stream.astype(jnp.float32)
    squares = lax.psum(jnp.sum(widened * widened, axis=1), ("tensor", "kv"))
    gain_mine = lax.dynamic_slice_in_dim(gain_wide, mine * width, width, 0)
    piece = (widened * lax.rsqrt(squares / D + epsilon)[:, None] * gain_mine[None, :]).astype(
        jnp.bfloat16
    )
    normed = lax.all_gather(piece, ("tensor", "kv"), axis=1, tiled=True)
    return (stream, normed)


def solution(mesh):
    placed = (
        P(("groups", "dp"), ("tensor", "kv")),
        P(("groups", "dp"), ("tensor", "kv")),
        P(None, ("groups", "dp"), None, None),
        P(None, ("groups", "dp"), ("tensor", "kv"), None, None),
        P(("groups", "dp")),
        P(("tensor", "kv"), None),
        P(),
    )
    return jax.shard_map(
        on_device,
        mesh=mesh,
        in_specs=placed,
        out_specs=(P(("groups", "dp"), ("tensor", "kv")), P(("groups", "dp"), None)),
        check_vma=False,
    )
```

profile of v0, /device:TPU:0, one launch (start us, length us, event | category | flops | bytes accessed | tf_op | source)
XLA Modules:
  0.0 155.4 jit_solution(17761867516999163748)
XLA Ops:
  7.2 7.0 %fusion.25 = (bf16[1,16,256,4,128]{4,3,2,1,0:T(4,128)(2,1)}, bf16[1,16,256,4,128]{4,3,2,1,0:T(4,128)(2,1)S(1)}) fusion(bf16[2,16,256,4,128]{4,3,2,1,0:T(4,128)(2,1)} %param.10), kind=kLoop, calls=%fused_computation.48 | loop fusion | bytes 16777216 | tf_op jit(solution)/shard_map/slice | solution.py:38
  14.2 15.9 %all_gather.6 = bf16[16,8192]{1,0:T(8,128)(2,1)S(1)} all-gather(bf16[16,1024]{1,0:T(8,128)(2,1)S(1)} %copy-done.2), channel_id=1, replica_groups=mesh['groups'=2,'tensor'=4,'dp'=2,'kv'=2] {'tensor','kv'}, dimensions={1}, use_global_device_ids=true | all-gather | bytes 294912 | tf_op jit(solution)/shard_map/all_gather | solution.py:25
  30.3 1.3 fusion.26
  31.6 0.4 fusion.4
  32.1 0.6 broadcast.100
  32.6 0.7 reduce.1
  33.3 0.7 reshape.118
  34.0 4.7 %all-to-all-start.2 = ((f32[8,1,128]{2,1,0:T(1,128)}), f32[8,1,128]{2,1,0:T(1,128)S(1)}, u32[]{:S(2)}, u32[]{:S(2)}) async-start(f32[8,1,128]{2,1,0:T(1,128)} %reshape.118), calls=%async_computation.2 | async-start | bytes 8192 | tf_op jit(solution)/shard_map/all_to_all | solution.py:44
  38.8 0.7 reduce.3
  39.5 0.7 reshape.116
  40.2 4.1 %all-to-all-done.2 = f32[8,1,128]{2,1,0:T(1,128)S(1)} async-done(((f32[8,1,128]{2,1,0:T(1,128)}), f32[8,1,128]{2,1,0:T(1,128)S(1)}, u32[]{:S(2)}, u32[]{:S(2)}) %all-to-all-start.2) | async-done | bytes 4128 | tf_op jit(solution)/shard_map/all_to_all | solution.py:44
  44.2 3.3 %all-to-all-start.1 = ((f32[8,1,128]{2,1,0:T(1,128)}), f32[8,1,128]{2,1,0:T(1,128)S(1)}, u32[]{:S(2)}, u32[]{:S(2)}) async-start(f32[8,1,128]{2,1,0:T(1,128)} %reshape.116), calls=%async_computation.1 | async-start | bytes 8192 | tf_op jit(solution)/shard_map/all_to_all | solution.py:43
  47.5 2.9 %fusion = f32[16,4,16,128]{3,2,1,0:T(8,128)S(1)} fusion(bf16[1,16,256,4,128]{4,3,2,1,0:T(4,128)(2,1)} %get-tuple-element.9, f32[16,4,16,256]{3,2,1,0:T(8,128)S(1)} %get-tuple-element.12, f32[16,4,16]{2,1,0:T(4,128)S(1)} %get-tuple-element.11, pred[16,256]{1,0:T(8,128)(4,1)S(1)} %broadcast_compare_fusion), kind=kOutput, calls=%fused_computation.1 | convolution fusion | flops 67633152 | bytes 5775360 | tf_op jit(solution)/shard_map/bgjp,bpgd->bgjd/dot_general | solution.py:38
  50.4 1.1 copy.34
  51.5 1.5 all-to-all-done.1
  53.0 3.5 %all-to-all-start = ((f32[1,16,64,128]{3,1,0,2:T(8,128)}), f32[1,16,64,128]{3,1,0,2:T(8,128)S(1)}, u32[]{:S(2)}, u32[]{:S(2)}) async-start(f32[1,16,64,128]{3,1,0,2:T(8,128)} %copy.34), calls=%async_computation | async-start | bytes 1048576 | tf_op jit(solution)/shard_map/all_to_all | solution.py:45
  56.6 0.2 convolution_bitcast_fusion
  56.9 0.1 fusion.14
  57.0 0.6 reduce.2
  57.7 0.1 reshape.119
  57.8 0.6 reduce.4
  58.4 0.1 reshape.117
  58.7 13.1 %all-to-all-done = f32[1,16,64,128]{3,1,0,2:T(8,128)S(1)} async-done(((f32[1,16,64,128]{3,1,0,2:T(8,128)}), f32[1,16,64,128]{3,1,0,2:T(8,128)S(1)}, u32[]{:S(2)}, u32[]{:S(2)}) %all-to-all-start) | async-done | bytes 524320 | tf_op jit(solution)/shard_map/all_to_all | solution.py:45
  71.9 0.2 multiply_reduce_fusion
  72.2 13.9 %fusion.15 = f32[16,16384]{1,0:T(8,128)} fusion(bf16[1024,16384]{1,0:T(8,128)(2,1)} %param.12, f32[2,8,8,128]{3,2,1,0:T(8,128)S(1)} %bitcast.90, f32[2,8,8,128]{3,2,1,0:T(8,128)S(1)} %bitcast.88, f32[2,8,8,128]{3,2,1,0:T(8,128)S(1)} %bitcast.89, f32[16,8,128]{2,0,1:T(8,128)S(1)} %multiply_reduce_fusion, f32[16,8]{0,1:T(8,128)S(1)} %get-tuple-element.5), kind=kOutput, calls=%fused_computation.28 | convolution fusion | flops 536952832 | bytes 34865664 | tf_op jit(solution)/shard_map/dot_general | solution.py:65
  86.2 0.7 dynamic-slice_convert_fusion
  86.9 31.0 %reduce-scatter.2.cloned.1.call-done = f32[16,2048]{1,0:T(8,128)} async-done(((f32[16,16384]{1,0:T(8,128)}), f32[16,2048]{1,0:T(8,128)}) %reduce-scatter.2.cloned.1.call-update) | async-done | bytes 131088 | tf_op jit(solution)/shard_map/reduce_scatter | solution.py:67
  117.9 1.0 fusion.8
  118.9 13.8 %psum.7 = f32[16]{0:T(128)S(1)} all-reduce(f32[16]{0:T(128)S(1)} %get-tuple-element.2), channel_id=1, replica_groups=mesh['groups'=2,'tensor'=4,'dp'=2,'kv'=2] {'tensor','kv'}, use_global_device_ids=true, to_apply=%region_8.9 | all-reduce | flops 16 | bytes 128 | tf_op jit(solution)/shard_map/psum | solution.py:70
  132.8 0.1 fusion.10
  132.9 14.9 %all_gather.7 = bf16[16,16384]{1,0:T(8,128)(2,1)S(1)} all-gather(bf16[16,2048]{1,0:T(8,128)(2,1)S(1)} %fusion.10), channel_id=1, replica_groups=mesh['groups'=2,'tensor'=4,'dp'=2,'kv'=2] {'tensor','kv'}, dimensions={1}, use_global_device_ids=true | all-gather | bytes 589824 | tf_op jit(solution)/shard_map/all_gather | solution.py:75
  147.8 0.8 copy.70
  (30 shorter events, 0.8 us)
Async XLA Ops:
  7.2 49.5 %copy-start = (bf16[2,16,4,128]{3,2,1,0:T(4,128)(2,1)S(1)}, bf16[2,16,4,128]{3,2,1,0:T(4,128)(2,1)}, u32[]{:S(2)}) copy-start(bf16[2,16,4,128]{3,2,1,0:T(4,128)(2,1)} %param.9) | copy-start | bytes 98308
  7.2 7.0 %copy-start.2 = (bf16[16,1024]{1,0:T(8,128)(2,1)S(1)}, bf16[16,1024]{1,0:T(8,128)(2,1)}, u32[]{:S(2)}) copy-start(bf16[16,1024]{1,0:T(8,128)(2,1)} %param.8) | copy-start | bytes 98308
  7.2 23.0 %copy-start.4 = (s32[16]{0:T(128)S(1)}, s32[16]{0:T(128)}, u32[]{:S(2)}) copy-start(s32[16]{0:T(128)} %param.11) | copy-start | bytes 196
  34.0 10.2 %all-to-all-start.2 = ((f32[8,1,128]{2,1,0:T(1,128)}), f32[8,1,128]{2,1,0:T(1,128)S(1)}, u32[]{:S(2)}, u32[]{:S(2)}) async-start(f32[8,1,128]{2,1,0:T(1,128)} %reshape.118), calls=%async_computation.2 | async-start | bytes 8192 | tf_op jit(solution)/shard_map/all_to_all | solution.py:44
  44.2 8.8 %all-to-all-start.1 = ((f32[8,1,128]{2,1,0:T(1,128)}), f32[8,1,128]{2,1,0:T(1,128)S(1)}, u32[]{:S(2)}, u32[]{:S(2)}) async-start(f32[8,1,128]{2,1,0:T(1,128)} %reshape.116), calls=%async_computation.1 | async-start | bytes 8192 | tf_op jit(solution)/shard_map/all_to_all | solution.py:43
  53.0 18.9 %all-to-all-start = ((f32[1,16,64,128]{3,1,0,2:T(8,128)}), f32[1,16,64,128]{3,1,0,2:T(8,128)S(1)}, u32[]{:S(2)}, u32[]{:S(2)}) async-start(f32[1,16,64,128]{3,1,0,2:T(8,128)} %copy.34), calls=%async_computation | async-start | bytes 1048576 | tf_op jit(solution)/shard_map/all_to_all | solution.py:45
  56.5 61.3 %reduce-scatter.2.cloned.1.call-start = ((), (), s32[]{:S(2)}) async-start(), calls=%async_computation.4 | async-start | bytes 1179648 | tf_op jit(solution)/shard_map/reduce_scatter | solution.py:67
  72.2 45.7 %copy-start.3 = (bf16[16,2048]{1,0:T(8,128)(2,1)S(1)}, bf16[16,2048]{1,0:T(8,128)(2,1)}, u32[]{:S(2)}) copy-start(bf16[16,2048]{1,0:T(8,128)(2,1)} %param.7) | copy-start | bytes 196612
  118.9 29.7 %copy-start.1 = (bf16[16,2048]{1,0:T(8,128)(2,1)}, bf16[16,2048]{1,0:T(8,128)(2,1)S(1)}, u32[]{:S(2)}) copy-start(bf16[16,2048]{1,0:T(8,128)(2,1)S(1)} %get-tuple-element.15) | copy-start | bytes 196612
Sparse Core Ops, SparseCore 0:
  86.3 31.5 reduce-scatter.1
where the time goes:
time: 156 us; the launch traced here: 155 us
  waiting for transfers between devices  49.7 us (32%)
  blocking collectives  44.7 us (29%)
  matrix products  18.3 us (12%)
  between operations  14.2 us (9%)
  local copies, waits for them, and re-layouts  11.7 us (8%)
  starting transfers between devices  11.5 us (7%)
  other arithmetic  5.32 us (3%)
    reduce_scatter x1, waiting for transfers between devices, on_device(): lax.psum_scatter(partial_value, ('tensor', 'kv'), scatter_dimension=1, ti...  31 us
    all_gather x1, blocking collectives, on_device(): queries = lax.all_gather(query, ('tensor', 'kv'), axis=1, tiled=True)  15.9 us
    all_gather x1, blocking collectives, on_device(): normed = lax.all_gather(piece, ('tensor', 'kv'), axis=1, tiled=True)  14.9 us
    dot_general x1, matrix products, on_device(): jnp.dot(attended, out_weight, preferred_element_type=jnp.float32)  13.9 us
    psum x1, blocking collectives, on_device(): squares = lax.psum(jnp.sum(widened * widened, axis=1), ('tensor', 'kv'))  13.8 us
    all_to_all x1, waiting for transfers between devices, on_device(): lax.all_to_all(accum[None], ('tensor', 'kv'), split_axis=2, concat_axis=0...  13.1 us
    slice x1, local copies, waits for them, and re-layouts, on_device(): kv_cache[1]  7.01 us
    all_to_all x1, starting transfers between devices, on_device(): lax.all_to_all(totals[None], ('tensor', 'kv'), split_axis=2, concat_axis=...  4.68 us
  transfers between devices with their start and end apart: 4, of which 4 were waited for; matrix products, arithmetic and copies ran while one was open for 5% of the time, Pallas kernels for 0%

commit v1 on v0

v1 whole, which is shorter than its diff:
```python
import functools
import math

import jax
import jax.numpy as jnp
from jax import lax
from jax.experimental import pallas as pl
from jax.experimental.pallas import tpu as pltpu
from jax.sharding import PartitionSpec as P

HD = 128
LANES = 128
floor_value = -1e30
epsilon = 1e-05
MESH = pl.DeviceIdType.MESH


def kernel(
    T, K, kvh,
    lens_ref, q_ref, pair_ref, kv_hbm, w_hbm, res_ref, gain_ref,
    stream_ref, out_ref,
    kv, wbuf, qg, qf, of, lf, colid, abuf, arecv, fpart, pbuf, precv, zbuf, zrecv, full, lhs,
    kv_sem, w_sem, qs, qr, qfs, qfr, asend, ars, ps, pr, zs, zr, gs, gr, gfs, gfr,
):
    t = lax.axis_index("tensor")
    k = lax.axis_index("kv")
    n = T * K
    mine = t * K + k
    other = K - 1 - k
    S, width = res_ref.shape
    ph = q_ref.shape[1] // HD
    QH = ph * n
    group = QH // kvh
    C = kv.shape[2]
    span = C // kvh
    D = out_ref.shape[1]

    def kv_copy(i, b):
        return pltpu.make_async_copy(kv_hbm.at[i, b], kv.at[i, b], kv_sem.at[i, b])

    @pl.loop(0, S)
    def _(b):
        kv_copy(0, b).start()
        kv_copy(1, b).start()

    def hop(s):
        return lax.rem(t + 1 + s, T)

    def origin(s):
        return lax.rem(t + T - 1 - s, T)

    def w_copy(s):
        if s < T:
            dest = hop(s) * K + other
        else:
            dest = hop(s - T) * K + k
        cols = pl.ds(pl.multiple_of(dest * width, width), width)
        return pltpu.make_async_copy(w_hbm.at[:, cols], wbuf.at[s], w_sem.at[s])

    for s in range(n):
        w_copy(s).start()

    barrier = pltpu.get_barrier_semaphore()
    for p in range(1, n):
        j = lax.rem(mine + p, n)
        pl.semaphore_signal(
            barrier, inc=1, device_id={"tensor": j // K, "kv": lax.rem(j, K)}, device_id_type=MESH
        )
    qg[mine] = q_ref[...]
    pl.semaphore_wait(barrier, n - 1)

    def remote(src, dst, ss, rs, tt, kk):
        return pltpu.make_async_remote_copy(
            src_ref=src, dst_ref=dst, send_sem=ss, recv_sem=rs,
            device_id={"tensor": tt, "kv": kk}, device_id_type=MESH,
        )

    def gather_start(buf, ss, rs):
        out = []
        for s in range(T - 1):
            c = remote(buf.at[mine], buf.at[mine], ss.at[s], rs.at[s], hop(s), k)
            c.start()
            out.append(c)
        c = remote(buf.at[mine], buf.at[mine], ss.at[T - 1], rs.at[T - 1], t, other)
        c.start()
        out.append(c)
        return out

    def gather_finish(buf, copies, fs, fr):
        fwd = []
        order = sorted(range(T - 1), key=lambda s: min(s + 1, T - 1 - s))
        for s in order:
            copies[s].wait_recv()
            j = origin(s) * K + k
            c = remote(buf.at[j], buf.at[j], fs.at[s], fr.at[s], t, other)
            c.start()
            fwd.append(c)
        copies[T - 1].wait_recv()
        for c in fwd:
            c.wait_recv()
        return fwd

    qcopies = gather_start(qg, qs, qr)

    col = lax.broadcasted_iota(jnp.int32, (QH, C), 1)
    head = lax.broadcasted_iota(jnp.int32, (QH, C), 0)
    colid[...] = jnp.where(lax.rem(col, kvh) == head // group, col, jnp.int32(2**30))
    scale2 = math.log2(math.e) / math.sqrt(HD)
    my_group = (mine * ph) // group
    fkey = jnp.zeros((S, HD), jnp.float32)
    fval = jnp.zeros((S, HD), jnp.float32)
    for g in range(kvh):
        lanes = slice(g * HD, (g + 1) * HD)
        fkey = jnp.where(my_group == g, pair_ref[0, :, lanes].astype(jnp.float32), fkey)
        fval = jnp.where(my_group == g, pair_ref[1, :, lanes].astype(jnp.float32), fval)
    lane = lax.broadcasted_iota(jnp.int32, (S, LANES), 1)
    fresh = jnp.zeros((S, LANES), jnp.float32)
    for h in range(ph):
        prod = q_ref[:, h * HD:(h + 1) * HD].astype(jnp.float32) * fkey
        fresh = jnp.where(lane == h, jnp.sum(prod, axis=1, keepdims=True) * scale2, fresh)
    fpart[0] = fresh
    fpart[1] = fval

    qfwd = gather_finish(qg, qcopies, qfs, qfr)
    for j in range(n):
        for h in range(ph):
            r = (j * ph + h) * S
            qf[r:r + S, :] = qg[j, :, h * HD:(h + 1) * HD].astype(jnp.float32)

    start = mine * span

    def attend(b, _):
        kv_copy(0, b).wait()
        kv_copy(1, b).wait()
        qb = qf[pl.ds(b, QH, stride=S), :].astype(jnp.bfloat16)
        s = lax.dot_general(qb, kv[0, b], (((1,), (1,)), ((), ())), preferred_element_type=jnp.float32)
        lim = (lens_ref[b] - start) * kvh
        s = jnp.where(colid[...] < lim, s * scale2, floor_value)
        m = jnp.maximum(jnp.max(s, axis=1, keepdims=True), -1e29)
        p = jnp.exp2(s - m)
        l = jnp.maximum(jnp.sum(p, axis=1, keepdims=True), 1.0)
        o = jnp.dot(p.astype(jnp.bfloat16), kv[1, b], preferred_element_type=jnp.float32)
        of[pl.ds(b, QH, stride=S), :] = o / l
        lf[pl.ds(b, QH, stride=S), :] = jnp.broadcast_to(m + jnp.log2(l), (QH, LANES))
        return 0

    lax.fori_loop(0, S, attend, 0)

    low = lax.rem(lane, 32)
    for j in range(n):
        tot = jnp.zeros((S, LANES), jnp.float32)
        for h in range(ph):
            r = (j * ph + h) * S
            abuf[j, :, h * HD:(h + 1) * HD] = of[r:r + S, :].astype(jnp.bfloat16)
            tot = jnp.where(low == h, lf[r:r + S, :], tot)
        hi = tot.astype(jnp.bfloat16).astype(jnp.float32)
        mid = (tot - hi).astype(jnp.bfloat16).astype(jnp.float32)
        rest = tot - hi - mid
        packed = jnp.where(lane < 32, hi, jnp.where(lane < 64, mid, rest))
        abuf[j, :, ph * HD:] = packed.astype(jnp.bfloat16)
    acopies = []
    for p in range(1, n):
        j = lax.rem(mine + p, n)
        c = remote(abuf.at[j], arecv.at[mine], asend.at[p], ars.at[p], j // K, lax.rem(j, K))
        c.start()
        acopies.append(c)
    arecv[mine] = abuf[mine]
    for c in acopies:
        c.wait_recv()

    fresh = fpart[0]
    lse = []
    best = fresh
    for j in range(n):
        e = arecv[j, :, ph * HD:].astype(jnp.float32)
        e = e + pltpu.roll(e, 96, 1) + pltpu.roll(e, 64, 1)
        lse.append(e)
        best = jnp.maximum(best, e)
    fw = jnp.exp2(fresh - best)
    total = fw
    ws = []
    for j in range(n):
        w = jnp.exp2(lse[j] - best)
        ws.append(w)
        total = total + w
    inv = 1.0 / total
    for h in range(ph):
        acc = (fw * inv)[:, h:h + 1] * fpart[1]
        for j in range(n):
            acc = acc + (ws[j] * inv)[:, h:h + 1] * arecv[j, :, h * HD:(h + 1) * HD].astype(jnp.float32)
        lhs[:, h * HD:(h + 1) * HD] = acc.astype(jnp.bfloat16)

    tile = min(width, 512)

    pcopies = []
    for s in range(T):
        w_copy(s).wait()

        @pl.loop(0, width // tile)
        def _(i):
            cols = pl.ds(pl.multiple_of(i * tile, tile), tile)
            y = jnp.dot(lhs[...], wbuf[s, :, cols], preferred_element_type=jnp.float32)
            pbuf[s, :, cols] = y.astype(jnp.bfloat16)

        c = remote(pbuf.at[s], precv.at[s], ps.at[s], pr.at[s], t, other)
        c.start()
        pcopies.append(c)
    zcopies = []
    for s in range(T):
        w_copy(T + s).wait()
        pcopies[s].wait_recv()

        @pl.loop(0, width // tile)
        def _(i):
            cols = pl.ds(pl.multiple_of(i * tile, tile), tile)
            y = jnp.dot(lhs[...], wbuf[T + s, :, cols], preferred_element_type=jnp.float32)
            y = y + precv[s, :, cols].astype(jnp.float32)
            if s < T - 1:
                zbuf[s, :, cols] = y.astype(jnp.bfloat16)
            else:
                out = y + res_ref[:, cols].astype(jnp.float32)
                for u in range(tile // LANES):
                    qf[pl.ds(pl.multiple_of((i * (tile // LANES) + u) * S, S), S), :] = (
                        out[:, u * LANES:(u + 1) * LANES]
                    )

        if s < T - 1:
            c = remote(zbuf.at[s], zrecv.at[s], zs.at[s], zr.at[s], hop(s), k)
            c.start()
            zcopies.append(c)
    for c in zcopies:
        c.wait_recv()
    for u in range(width // LANES):
        cols = slice(u * LANES, (u + 1) * LANES)
        x = qf[u * S:(u + 1) * S, :]
        for s in range(T - 1):
            x = x + zrecv[s, :, cols].astype(jnp.float32)
        x = x.astype(jnp.bfloat16)
        full[mine, :, cols] = x
        stream_ref[:, cols] = x

    gcopies = gather_start(full, gs, gr)
    gfwd = gather_finish(full, gcopies, gfs, gfr)

    sq = jnp.zeros((S, width), jnp.float32)
    for j in range(n):
        x = full[j].astype(jnp.float32)
        sq = sq + x * x
    r = lax.rsqrt(jnp.sum(sq, axis=1, keepdims=True) / D + epsilon)
    for j in range(n):
        cols = slice(j * width, (j + 1) * width)
        x = full[j].astype(jnp.float32) * r * gain_ref[:, cols].astype(jnp.float32)
        out_ref[:, cols] = x.astype(jnp.bfloat16)

    for c in qcopies + qfwd + acopies + pcopies + zcopies + gcopies + gfwd:
        c.wait_send()


def on_device(T, K, residual, query, new_pair, kv_cache, lengths, out_weight, norm_gain):
    n = T * K
    S, width = residual.shape
    ph = query.shape[1] // HD
    span, kvh = kv_cache.shape[2:4]
    C = span * kvh
    QH = ph * n
    D = out_weight.shape[1]
    vm = pl.BlockSpec(memory_space=pltpu.VMEM)
    hbm = pl.BlockSpec(memory_space=pl.ANY)
    bf = jnp.bfloat16
    dma = pltpu.SemaphoreType.DMA
    scratch = [
        pltpu.VMEM((2, S, C, HD), bf),
        pltpu.VMEM((n, ph * HD, width), bf),
        pltpu.VMEM((n, S, ph * HD), bf),
        pltpu.VMEM((QH * S, HD), jnp.float32),
        pltpu.VMEM((QH * S, HD), jnp.float32),
        pltpu.VMEM((QH * S, LANES), jnp.float32),
        pltpu.VMEM((QH, C), jnp.int32),
        pltpu.VMEM((n, S, (ph + 1) * HD), bf),
        pltpu.VMEM((n, S, (ph + 1) * HD), bf),
        pltpu.VMEM((2, S, LANES), jnp.float32),
        pltpu.VMEM((T, S, width), bf),
        pltpu.VMEM((T, S, width), bf),
        pltpu.VMEM((T, S, width), bf),
        pltpu.VMEM((T, S, width), bf),
        pltpu.VMEM((n, S, width), bf),
        pltpu.VMEM((S, ph * HD), bf),
        dma((2, S)),
        dma((n,)),
        dma((T,)), dma((T,)), dma((T,)), dma((T,)),
        dma((n,)), dma((n,)),
        dma((T,)), dma((T,)),
        dma((T,)), dma((T,)),
        dma((T,)), dma((T,)), dma((T,)), dma((T,)),
    ]
    return pl.pallas_call(
        functools.partial(kernel, T, K, kvh),
        out_shape=(
            jax.ShapeDtypeStruct((S, width), bf),
            jax.ShapeDtypeStruct((S, D), bf),
        ),
        in_specs=[pl.BlockSpec(memory_space=pltpu.SMEM), vm, vm, hbm, hbm, vm, vm],
        out_specs=(vm, vm),
        scratch_shapes=scratch,
        compiler_params=pltpu.CompilerParams(
            collective_id=0, has_side_effects=True, vmem_limit_bytes=60 * 1024 * 1024
        ),
    )(
        lengths,
        query,
        new_pair.reshape(2, S, kvh * HD),
        kv_cache.reshape(2, S, C, HD),
        out_weight,
        residual,
        norm_gain.reshape(1, D),
    )


def solution(mesh):
    T, K = mesh.shape["tensor"], mesh.shape["kv"]
    seqs = ("groups", "dp")
    split = ("tensor", "kv")
    placed = (
        P(seqs, split),
        P(seqs, split),
        P(None, seqs, None, None),
        P(None, seqs, split, None, None),
        P(seqs),
        P(split, None),
        P(),
    )
    return jax.shard_map(
        functools.partial(on_device, T, K),
        mesh=mesh,
        in_specs=placed,
        out_specs=(P(seqs, split), P(seqs, None)),
        check_vma=False,
    )
```

time: 156 us -> 55.4 us (0.36)
  waiting for transfers between devices: 49.7 us -> 0 us
  Pallas kernels: 0 us -> 48.1 us
  blocking collectives: 44.7 us -> 0 us
  matrix products: 18.3 us -> 0 us
  between operations: 14.2 us -> 0.64 us
  starting transfers between devices: 11.5 us -> 0 us
  local copies, waits for them, and re-layouts: 11.7 us -> 6.15 us
  other arithmetic: 5.32 us -> 0 us
    pallas_call x0 -> x1, Pallas kernels: none -> 48.1 us  [on_device(): pl.pallas_call(functools.partial(kernel, T, K, kvh), out_shape=(jax.Shape...]
    reduce_scatter x1 -> x0, waiting for transfers between devices: 31 us -> none  [on_device(): lax.psum_scatter(partial_value, ('tensor', 'kv'), scatter_dimension=1, ti...]
    all_gather x2 -> x0, blocking collectives: 30.8 us -> none  [the longest x1 15.9 us: on_device(): queries = lax.all_gather(query, ('tensor', 'kv'), axis=1, tiled=True)]
    all_to_all x3 -> x0, waiting for transfers between devices: 18.7 us -> none  [the longest x1 13.1 us: on_device(): lax.all_to_all(accum[None], ('tensor', 'kv'), split_axis=2, concat_axis=0...]
    dot_general x4 -> x0, matrix products: 18.3 us -> none  [the longest x1 13.9 us: on_device(): jnp.dot(attended, out_weight, preferred_element_type=jnp.float32)]
    psum x1 -> x0, blocking collectives: 13.8 us -> none  [on_device(): squares = lax.psum(jnp.sum(widened * widened, axis=1), ('tensor', 'kv'))]
    all_to_all x3 -> x0, starting transfers between devices: 11.5 us -> none  [the longest x1 4.68 us: on_device(): lax.all_to_all(totals[None], ('tensor', 'kv'), split_axis=2, concat_axis=...]
    slice x2 -> x0, local copies, waits for them, and re-layouts: 7.02 us -> none  [the longest x1 7.01 us: on_device(): kv_cache[1]]
  transfers between devices with their start and end apart: 4 -> 0, of which waited for: 4 -> 0; matrix products, arithmetic and copies ran while one was open for 5% -> 0% of each run, Pallas kernels for 0% -> 0%
where the time goes in v1:
time: 55.4 us; the launch traced here: 54.9 us
  Pallas kernels  48.1 us (87%)
  local copies, waits for them, and re-layouts  6.15 us (11%)
  between operations  0.64 us (1%)
    pallas_call x1, Pallas kernels, on_device(): pl.pallas_call(functools.partial(kernel, T, K, kvh), out_shape=(jax.Shape...  48.1 us
    unnamed x2, local copies, waits for them, and re-layouts  3.34 us
    reshape x1, local copies, waits for them, and re-layouts, on_device(): norm_gain.reshape(1, D)  1.42 us
    reshape x1, local copies, waits for them, and re-layouts, on_device(): new_pair.reshape(2, S, kvh * HD)  1.39 us

profile of v1, /device:TPU:0, one launch (start us, length us, event | category | flops | bytes accessed | tf_op | source)
XLA Modules:
  0.0 54.9 jit_solution(14941248712259578142)
XLA Ops:
  0.6 1.4 %reshape.13.pair_ref = bf16[2,16,512]{2,1,0:T(8,128)(2,1)} reshape(bf16[2,16,4,128]{3,2,1,0:T(4,128)(2,1)} %param.9) | data formatting | bytes 65536 | tf_op jit(solution)/shard_map/reshape | solution.py:311
  2.0 1.4 %reshape.15.gain_ref = bf16[1,16384]{1,0:T(2,128)(2,1)} reshape(bf16[16384]{0:T(1024)(128)(2,1)} %param.13) | data formatting | bytes 65536 | tf_op jit(solution)/shard_map/reshape | solution.py:315
  3.4 48.1 %shard_map.86 = (bf16[16,2048]{1,0:T(8,128)(2,1)}, bf16[16,16384]{1,0:T(8,128)(2,1)}) custom-call(s32[16]{0:T(128)} %lens_ref.1, bf16[16,1024]{1,0:T(8,128)(2,1)} %q_ref.1, bf16[2,16,512]{2,1,0:T(8,128)(2,1)} %reshape.13.pair_ref, bf16[2,16,1024,128]{3,2,1,0:T(8,128)(2,1)} %bitcast.1, bf16[1024,16384]{1,0:T(8,128)(2,1)} %w_hbm.1, bf16[16,2048]{1,0:T(8,128)(2,1)} %res_ref.1, ...), custom_call_target="tpu_custom_call" | custom-call | tf_op jit(solution)/shard_map/pallas_call | solution.py:296
  51.5 1.5 %copy.11 = bf16[16,2048]{1,0:T(8,128)(2,1)} copy(bf16[16,2048]{1,0:T(8,128)(2,1)} %get-tuple-element.4) | data formatting | bytes 131072
  53.0 1.9 %copy.12 = bf16[16,16384]{1,0:T(8,128)(2,1)} copy(bf16[16,16384]{1,0:T(8,128)(2,1)} %get-tuple-element.5) | data formatting | bytes 1048576

commit v2 on v1

v2 whole, which is shorter than its diff:
```python
import functools
import math

import jax
import jax.numpy as jnp
from jax import lax
from jax.experimental import pallas as pl
from jax.experimental.pallas import tpu as pltpu
from jax.sharding import PartitionSpec as P

HD = 128
LANES = 128
floor_value = -1e30
epsilon = 1e-05
MESH = pl.DeviceIdType.MESH
VOUT = pltpu.VMEM


def kernel(
    T, K, kvh,
    lens_ref, q_hbm, pair_hbm, kv_hbm, w_hbm, res_hbm,
    stream_ref, full,
    pair_ref, res_ref, ybuf, kv, wbuf, qg, qf, of, lf, colid, abuf, arecv, fpart, pbuf, precv, zbuf, zrecv, lhs,
    small_sem, kv_sem, w_sem, qs, qr, qfs, qfr, asend, ars, ps, pr, zs, zr, gs, gr, gfs, gfr,
):
    t = lax.axis_index("tensor")
    k = lax.axis_index("kv")
    n = T * K
    mine = t * K + k
    other = K - 1 - k
    S, width = res_ref.shape
    ph = q_hbm.shape[1] // HD
    QH = ph * n
    group = QH // kvh
    C = kv.shape[2]
    span = C // kvh
    rows = S // 2

    barrier = pltpu.get_barrier_semaphore()
    for p in range(1, n):
        j = lax.rem(mine + p, n)
        pl.semaphore_signal(
            barrier, inc=1, device_id={"tensor": j // K, "kv": lax.rem(j, K)}, device_id_type=MESH
        )

    small = [
        pltpu.make_async_copy(q_hbm, qg.at[mine], small_sem.at[0]),
        pltpu.make_async_copy(pair_hbm, pair_ref, small_sem.at[1]),
        pltpu.make_async_copy(res_hbm, res_ref, small_sem.at[2]),
    ]
    for c in small:
        c.start()

    def kv_copy(i, b):
        return pltpu.make_async_copy(kv_hbm.at[i, b], kv.at[i, b], kv_sem.at[i, b])

    @pl.loop(0, S)
    def _(b):
        kv_copy(0, b).start()
        kv_copy(1, b).start()

    def hop(s):
        return lax.rem(t + 1 + s, T)

    def origin(s):
        return lax.rem(t + T - 1 - s, T)

    def w_copy(s):
        dest = hop(s // 2) * K + (k if s % 2 else other)
        cols = pl.ds(pl.multiple_of(dest * width, width), width)
        return pltpu.make_async_copy(w_hbm.at[:, cols], wbuf.at[s], w_sem.at[s])

    for s in range(n):
        w_copy(s).start()

    small[0].wait()
    pl.semaphore_wait(barrier, n - 1)

    def remote(src, dst, ss, rs, tt, kk):
        return pltpu.make_async_remote_copy(
            src_ref=src, dst_ref=dst, send_sem=ss, recv_sem=rs,
            device_id={"tensor": tt, "kv": kk}, device_id_type=MESH,
        )

    def gather_start(buf, ss, rs):
        out = []
        for s in range(T - 1):
            c = remote(buf.at[mine], buf.at[mine], ss.at[s], rs.at[s], hop(s), k)
            c.start()
            out.append(c)
        c = remote(buf.at[mine], buf.at[mine], ss.at[T - 1], rs.at[T - 1], t, other)
        c.start()
        out.append(c)
        return out

    def gather_finish(buf, copies, fs, fr):
        fwd = []
        order = sorted(range(T - 1), key=lambda s: min(s + 1, T - 1 - s))
        for s in order:
            copies[s].wait_recv()
            j = origin(s) * K + k
            c = remote(buf.at[j], buf.at[j], fs.at[s], fr.at[s], t, other)
            c.start()
            fwd.append(c)
        copies[T - 1].wait_recv()
        for c in fwd:
            c.wait_recv()
        return fwd

    qcopies = gather_start(qg, qs, qr)

    col = lax.broadcasted_iota(jnp.int32, (QH, C), 1)
    head = lax.broadcasted_iota(jnp.int32, (QH, C), 0)
    colid[...] = jnp.where(lax.rem(col, kvh) == head // group, col, jnp.int32(2**30))
    scale2 = math.log2(math.e) / math.sqrt(HD)
    my_group = (mine * ph) // group
    fkey = jnp.zeros((S, HD), jnp.float32)
    fval = jnp.zeros((S, HD), jnp.float32)
    small[1].wait()
    small[2].wait()
    for g in range(kvh):
        fkey = jnp.where(my_group == g, pair_ref[0, :, g, :].astype(jnp.float32), fkey)
        fval = jnp.where(my_group == g, pair_ref[1, :, g, :].astype(jnp.float32), fval)
    lane = lax.broadcasted_iota(jnp.int32, (S, LANES), 1)
    fresh = jnp.zeros((S, LANES), jnp.float32)
    for h in range(ph):
        prod = qg[mine, :, h * HD:(h + 1) * HD].astype(jnp.float32) * fkey
        fresh = jnp.where(lane == h, jnp.sum(prod, axis=1, keepdims=True) * scale2, fresh)
    fpart[0] = fresh
    fpart[1] = fval

    qfwd = gather_finish(qg, qcopies, qfs, qfr)
    for j in range(n):
        for h in range(ph):
            r = (j * ph + h) * S
            qf[r:r + S, :] = qg[j, :, h * HD:(h + 1) * HD].astype(jnp.float32)

    start = mine * span

    def attend(b, _):
        kv_copy(0, b).wait()
        kv_copy(1, b).wait()
        qb = qf[pl.ds(b, QH, stride=S), :].astype(jnp.bfloat16)
        s = lax.dot_general(qb, kv[0, b], (((1,), (1,)), ((), ())), preferred_element_type=jnp.float32)
        lim = (lens_ref[b] - start) * kvh
        s = jnp.where(colid[...] < lim, s * scale2, floor_value)
        m = jnp.maximum(jnp.max(s, axis=1, keepdims=True), -1e29)
        p = jnp.exp2(s - m)
        l = jnp.maximum(jnp.sum(p, axis=1, keepdims=True), 1.0)
        o = jnp.dot(p.astype(jnp.bfloat16), kv[1, b], preferred_element_type=jnp.float32)
        of[pl.ds(b, QH, stride=S), :] = o / l
        lf[pl.ds(b, QH, stride=S), :] = jnp.broadcast_to(m + jnp.log2(l), (QH, LANES))
        return 0

    lane = lax.broadcasted_iota(jnp.int32, (rows, LANES), 1)
    low = lax.rem(lane, 32)
    acopies = []
    for half in range(2):
        lax.fori_loop(half * rows, (half + 1) * rows, attend, 0, unroll=4)
        for j in range(n):
            tot = jnp.zeros((rows, LANES), jnp.float32)
            for h in range(ph):
                r = (j * ph + h) * S + half * rows
                abuf[half, j, :, h * HD:(h + 1) * HD] = of[r:r + rows, :].astype(jnp.bfloat16)
                tot = jnp.where(low == h, lf[r:r + rows, :], tot)
            hi = tot.astype(jnp.bfloat16).astype(jnp.float32)
            mid = (tot - hi).astype(jnp.bfloat16).astype(jnp.float32)
            rest = tot - hi - mid
            packed = jnp.where(lane < 32, hi, jnp.where(lane < 64, mid, rest))
            abuf[half, j, :, ph * HD:] = packed.astype(jnp.bfloat16)
        for p in range(1, n):
            j = lax.rem(mine + p, n)
            c = remote(
                abuf.at[half, j], arecv.at[half, mine], asend.at[half, p], ars.at[half, p],
                j // K, lax.rem(j, K),
            )
            c.start()
            acopies.append(c)
        arecv[half, mine] = abuf[half, mine]

    parts = []
    for half in range(2):
        for c in acopies[half * (n - 1):(half + 1) * (n - 1)]:
            c.wait_recv()
        fresh = fpart[0, half * rows:(half + 1) * rows, :]
        value = fpart[1, half * rows:(half + 1) * rows, :]
        lse = []
        best = fresh
        for j in range(n):
            e = arecv[half, j, :, ph * HD:].astype(jnp.float32)
            e = e + pltpu.roll(e, 96, 1) + pltpu.roll(e, 64, 1)
            lse.append(e)
            best = jnp.maximum(best, e)
        fw = jnp.exp2(fresh - best)
        total = fw
        ws = []
        for j in range(n):
            w = jnp.exp2(lse[j] - best)
            ws.append(w)
            total = total + w
        inv = 1.0 / total
        accs = []
        for h in range(ph):
            acc = (fw * inv)[:, h:h + 1] * value
            for j in range(n):
                acc = acc + (ws[j] * inv)[:, h:h + 1] * arecv[half, j, :, h * HD:(h + 1) * HD].astype(jnp.float32)
            accs.append(acc)
        parts.append(accs)
    for h in range(ph):
        both = jnp.concatenate([parts[0][h], parts[1][h]], axis=0)
        lhs[:, h * HD:(h + 1) * HD] = both.astype(jnp.bfloat16)

    pcopies, zcopies = [], []
    for s in range(T):
        w_copy(2 * s).wait()
        y = jnp.dot(lhs[...], wbuf[2 * s], preferred_element_type=jnp.float32)
        pbuf[s] = y.astype(jnp.bfloat16)
        c = remote(pbuf.at[s], precv.at[s], ps.at[s], pr.at[s], t, other)
        c.start()
        pcopies.append(c)
        w_copy(2 * s + 1).wait()
        ybuf[...] = jnp.dot(lhs[...], wbuf[2 * s + 1], preferred_element_type=jnp.float32)
        c.wait_recv()
        if s < T - 1:
            zbuf[s] = (ybuf[...] + precv[s].astype(jnp.float32)).astype(jnp.bfloat16)
            c = remote(zbuf.at[s], zrecv.at[s], zs.at[s], zr.at[s], hop(s), k)
            c.start()
            zcopies.append(c)
        else:
            ybuf[...] += precv[s].astype(jnp.float32) + res_ref[...].astype(jnp.float32)
    for c in zcopies:
        c.wait_recv()
    total = ybuf[...]
    for s in range(T - 1):
        total = total + zrecv[s].astype(jnp.float32)
    x = total.astype(jnp.bfloat16)
    full[mine] = x
    stream_ref[...] = x

    gcopies = gather_start(full, gs, gr)
    gfwd = gather_finish(full, gcopies, gfs, gfr)

    for c in qcopies + qfwd + acopies + pcopies + zcopies + gcopies + gfwd:
        c.wait_send()


def norm_kernel(part_ref, full_ref, gain_ref, stream_ref, out_ref):
    n, S, width = full_ref.shape
    stream_ref[...] = part_ref[...]
    sq = jnp.zeros((S, width), jnp.float32)
    for j in range(n):
        x = full_ref[j].astype(jnp.float32)
        sq = sq + x * x
    r = lax.rsqrt(jnp.sum(sq, axis=1, keepdims=True) / (n * width) + epsilon)
    for j in range(n):
        cols = slice(j * width, (j + 1) * width)
        gain = gain_ref[cols].astype(jnp.float32).reshape(1, width)
        out_ref[:, cols] = (full_ref[j].astype(jnp.float32) * r * gain).astype(jnp.bfloat16)


def on_device(T, K, residual, query, new_pair, kv_cache, lengths, out_weight, norm_gain):
    n = T * K
    S, width = residual.shape
    ph = query.shape[1] // HD
    span, kvh = kv_cache.shape[2:4]
    C = span * kvh
    QH = ph * n
    D = out_weight.shape[1]
    vm = pl.BlockSpec(memory_space=pltpu.VMEM)
    hbm = pl.BlockSpec(memory_space=pl.ANY)
    bf = jnp.bfloat16
    dma = pltpu.SemaphoreType.DMA
    rows = S // 2
    scratch = [
        pltpu.VMEM((2, S, kvh, HD), bf),
        pltpu.VMEM((S, width), bf),
        pltpu.VMEM((S, width), jnp.float32),
        pltpu.VMEM((2, S, C, HD), bf),
        pltpu.VMEM((n, ph * HD, width), bf),
        pltpu.VMEM((n, S, ph * HD), bf),
        pltpu.VMEM((QH * S, HD), jnp.float32),
        pltpu.VMEM((QH * S, HD), jnp.float32),
        pltpu.VMEM((QH * S, LANES), jnp.float32),
        pltpu.VMEM((QH, C), jnp.int32),
        pltpu.VMEM((2, n, rows, (ph + 1) * HD), bf),
        pltpu.VMEM((2, n, rows, (ph + 1) * HD), bf),
        pltpu.VMEM((2, S, LANES), jnp.float32),
        pltpu.VMEM((T, S, width), bf),
        pltpu.VMEM((T, S, width), bf),
        pltpu.VMEM((T, S, width), bf),
        pltpu.VMEM((T, S, width), bf),
        pltpu.VMEM((S, ph * HD), bf),
        dma((3,)),
        dma((2, S)),
        dma((n,)),
        dma((T,)), dma((T,)), dma((T,)), dma((T,)),
        dma((2, n)), dma((2, n)),
        dma((T,)), dma((T,)),
        dma((T,)), dma((T,)),
        dma((T,)), dma((T,)), dma((T,)), dma((T,)),
    ]
    part, full = pl.pallas_call(
        functools.partial(kernel, T, K, kvh),
        out_shape=(VOUT((S, width), bf), VOUT((n, S, width), bf)),
        in_specs=[pl.BlockSpec(memory_space=pltpu.SMEM)] + [hbm] * 5,
        out_specs=(vm, vm),
        scratch_shapes=scratch,
        compiler_params=pltpu.CompilerParams(
            collective_id=0, has_side_effects=True, vmem_limit_bytes=58 * 1024 * 1024
        ),
    )(lengths, query, new_pair, kv_cache.reshape(2, S, C, HD), out_weight, residual)
    return pl.pallas_call(
        norm_kernel,
        out_shape=(jax.ShapeDtypeStruct((S, width), bf), jax.ShapeDtypeStruct((S, D), bf)),
        in_specs=[vm, vm, vm],
        out_specs=(vm, vm),
        compiler_params=pltpu.CompilerParams(vmem_limit_bytes=8 * 1024 * 1024),
    )(part, full, norm_gain)


def solution(mesh):
    T, K = mesh.shape["tensor"], mesh.shape["kv"]
    seqs = ("groups", "dp")
    split = ("tensor", "kv")
    placed = (
        P(seqs, split),
        P(seqs, split),
        P(None, seqs, None, None),
        P(None, seqs, split, None, None),
        P(seqs),
        P(split, None),
        P(),
    )
    return jax.shard_map(
        functools.partial(on_device, T, K),
        mesh=mesh,
        in_specs=placed,
        out_specs=(P(seqs, split), P(seqs, None)),
        check_vma=False,
    )
```

time: 55.4 us -> 43.8 us (0.79)
  local copies, waits for them, and re-layouts: 6.15 us -> 0.01 us
  Pallas kernels: 48.1 us -> 43 us
    pallas_call x1 -> x2, Pallas kernels: 48.1 us -> 43 us  [the longest x1 41.8 us: on_device(): pl.pallas_call(functools.partial(kernel, T, K, kvh), out_shape=(VOUT((S,...]
    unnamed x2, local copies, waits for them, and re-layouts: 3.34 us -> 0.01 us
    reshape x2 -> x0, local copies, waits for them, and re-layouts: 2.81 us -> none  [the longest x1 1.42 us: on_device(): norm_gain.reshape(1, D)]
where the time goes in v2:
time: 43.8 us; the launch traced here: 43.6 us
  Pallas kernels  43 us (98%)
  between operations  0.66 us (2%)
    pallas_call x1, Pallas kernels, on_device(): pl.pallas_call(functools.partial(kernel, T, K, kvh), out_shape=(VOUT((S,...  41.8 us
    pallas_call x1, Pallas kernels, on_device(): pl.pallas_call(norm_kernel, out_shape=(jax.ShapeDtypeStruct((S, width), b...  1.17 us

profile of v2, /device:TPU:0, one launch (start us, length us, event | category | flops | bytes accessed | tf_op | source)
XLA Modules:
  0.0 43.6 jit_solution(12682012236012409494)
XLA Ops:
  0.6 0.0 copy-start
  0.6 41.8 %shard_map.86 = (bf16[16,2048]{1,0:T(8,128)(2,1)S(1)}, bf16[8,16,2048]{2,1,0:T(8,128)(2,1)S(1)}) custom-call(s32[16]{0:T(128)} %lens_ref.1, bf16[16,1024]{1,0:T(8,128)(2,1)} %q_hbm.1, bf16[2,16,4,128]{3,2,1,0:T(4,128)(2,1)} %pair_hbm.1, bf16[2,16,1024,128]{3,2,1,0:T(8,128)(2,1)} %bitcast.1, bf16[1024,16384]{1,0:T(8,128)(2,1)} %w_hbm.1, bf16[16,2048]{1,0:T(8,128)(2,1)} %res_hbm.1), custom_call_target="tpu_custom_call" | custom-call | tf_op jit(solution)/shard_map/pallas_call | solution.py:302
  42.4 0.0 copy-done
  42.5 1.2 %shard_map.87 = (bf16[16,2048]{1,0:T(8,128)(2,1)}, bf16[16,16384]{1,0:T(8,128)(2,1)}) custom-call(bf16[16,2048]{1,0:T(8,128)(2,1)S(1)} %get-tuple-element.4.part_ref, bf16[8,16,2048]{2,1,0:T(8,128)(2,1)S(1)} %get-tuple-element.5.full_ref, bf16[16384]{0:T(1024)(128)(2,1)S(1)} %copy-done), custom_call_target="tpu_custom_call" | custom-call | tf_op jit(solution)/shard_map/pallas_call | solution.py:312
Async XLA Ops:
  0.6 41.8 %copy-start = (bf16[16384]{0:T(1024)(128)(2,1)S(1)}, bf16[16384]{0:T(1024)(128)(2,1)}, u32[]{:S(2)}) copy-start(bf16[16384]{0:T(1024)(128)(2,1)} %gain_ref.1) | copy-start | bytes 98308

commit v3 on v2

--- a/solution.py
+++ b/solution.py
@@ -35,6 +35,7 @@
     C = kv.shape[2]
     span = C // kvh
     rows = S // 2
+    hw = width // 2
 
     barrier = pltpu.get_barrier_semaphore()
     for p in range(1, n):
@@ -82,24 +83,24 @@
             device_id={"tensor": tt, "kv": kk}, device_id_type=MESH,
         )
 
-    def gather_start(buf, ss, rs):
+    def gather_start(view, ss, rs):
         out = []
         for s in range(T - 1):
-            c = remote(buf.at[mine], buf.at[mine], ss.at[s], rs.at[s], hop(s), k)
+            c = remote(view(mine), view(mine), ss.at[s], rs.at[s], hop(s), k)
             c.start()
             out.append(c)
-        c = remote(buf.at[mine], buf.at[mine], ss.at[T - 1], rs.at[T - 1], t, other)
+        c = remote(view(mine), view(mine), ss.at[T - 1], rs.at[T - 1], t, other)
         c.start()
         out.append(c)
         return out
 
-    def gather_finish(buf, copies, fs, fr):
+    def gather_finish(view, copies, fs, fr):
         fwd = []
         order = sorted(range(T - 1), key=lambda s: min(s + 1, T - 1 - s))
         for s in order:
             copies[s].wait_recv()
             j = origin(s) * K + k
-            c = remote(buf.at[j], buf.at[j], fs.at[s], fr.at[s], t, other)
+            c = remote(view(j), view(j), fs.at[s], fr.at[s], t, other)
             c.start()
             fwd.append(c)
         copies[T - 1].wait_recv()
@@ -107,7 +108,7 @@
             c.wait_recv()
         return fwd
 
-    qcopies = gather_start(qg, qs, qr)
+    qcopies = gather_start(lambda j: qg.at[j], qs, qr)
 
     col = lax.broadcasted_iota(jnp.int32, (QH, C), 1)
     head = lax.broadcasted_iota(jnp.int32, (QH, C), 0)
@@ -129,7 +130,7 @@
     fpart[0] = fresh
     fpart[1] = fval
 
-    qfwd = gather_finish(qg, qcopies, qfs, qfr)
+    qfwd = gather_finish(lambda j: qg.at[j], qcopies, qfs, qfr)
     for j in range(n):
         for h in range(ph):
             r = (j * ph + h) * S
@@ -211,34 +212,54 @@
         lhs[:, h * HD:(h + 1) * HD] = both.astype(jnp.bfloat16)
 
     pcopies, zcopies = [], []
-    for s in range(T):
-        w_copy(2 * s).wait()
-        y = jnp.dot(lhs[...], wbuf[2 * s], preferred_element_type=jnp.float32)
-        pbuf[s] = y.astype(jnp.bfloat16)
-        c = remote(pbuf.at[s], precv.at[s], ps.at[s], pr.at[s], t, other)
-        c.start()
-        pcopies.append(c)
-        w_copy(2 * s + 1).wait()
-        ybuf[...] = jnp.dot(lhs[...], wbuf[2 * s + 1], preferred_element_type=jnp.float32)
-        c.wait_recv()
-        if s < T - 1:
-            zbuf[s] = (ybuf[...] + precv[s].astype(jnp.float32)).astype(jnp.bfloat16)
-            c = remote(zbuf.at[s], zrecv.at[s], zs.at[s], zr.at[s], hop(s), k)
+
+    def project(half):
+        cols = slice(half * hw, (half + 1) * hw)
+        for s in range(T):
+            if half == 0:
+                w_copy(2 * s).wait()
+            y = jnp.dot(lhs[...], wbuf[2 * s, :, cols], preferred_element_type=jnp.float32)
+            pbuf[half, s] = y.astype(jnp.bfloat16)
+            c = remote(pbuf.at[half, s], precv.at[half, s], ps.at[half, s], pr.at[half, s], t, other)
             c.start()
-            zcopies.append(c)
-        else:
-            ybuf[...] += precv[s].astype(jnp.float32) + res_ref[...].astype(jnp.float32)
-    for c in zcopies:
-        c.wait_recv()
-    total = ybuf[...]
-    for s in range(T - 1):
-        total = total + zrecv[s].astype(jnp.float32)
-    x = total.astype(jnp.bfloat16)
-    full[mine] = x
-    stream_ref[...] = x
-
-    gcopies = gather_start(full, gs, gr)
-    gfwd = gather_finish(full, gcopies, gfs, gfr)
+            pcopies.append(c)
+            if half == 0:
+                w_copy(2 * s + 1).wait()
+            ybuf[half] = jnp.dot(lhs[...], wbuf[2 * s + 1, :, cols], preferred_element_type=jnp.float32)
+            c.wait_recv()
+            y = ybuf[half] + precv[half, s].astype(jnp.float32)
+            if s < T - 1:
+                zbuf[half, s] = y.astype(jnp.bfloat16)
+                c = remote(zbuf.at[half, s], zrecv.at[half, s], zs.at[half, s], zr.at[half, s], hop(s), k)
+                c.start()
+                zcopies.append(c)
+            else:
+                ybuf[half] = y + res_ref[:, cols].astype(jnp.float32)
+
+    gcopies, gfwd = [], []
+
+    def view(half):
+        return lambda j: full.at[j, :, pl.ds(half * hw, hw)]
+
+    def settle(half):
+        cols = slice(half * hw, (half + 1) * hw)
+        for c in zcopies[half * (T - 1):(half + 1) * (T - 1)]:
+            c.wait_recv()
+        total = ybuf[half]
+        for s in range(T - 1):
+            total = total + zrecv[half, s].astype(jnp.float32)
+        x = total.astype(jnp.bfloat16)
+        full[mine, :, cols] = x
+        stream_ref[:, cols] = x
+        gcopies.extend(gather_start(view(half), gs.at[half], gr.at[half]))
+
+    project(0)
+    project(1)
+    settle(0)
+    settle(1)
+    for half in range(2):
+        mine_copies = gcopies[half * T:(half + 1) * T]
+        gfwd.extend(gather_finish(view(half), mine_copies, gfs.at[half], gfr.at[half]))
 
     for c in qcopies + qfwd + acopies + pcopies + zcopies + gcopies + gfwd:
         c.wait_send()
@@ -274,7 +295,7 @@
     scratch = [
         pltpu.VMEM((2, S, kvh, HD), bf),
         pltpu.VMEM((S, width), bf),
-        pltpu.VMEM((S, width), jnp.float32),
+        pltpu.VMEM((2, S, width // 2), jnp.float32),
         pltpu.VMEM((2, S, C, HD), bf),
         pltpu.VMEM((n, ph * HD, width), bf),
         pltpu.VMEM((n, S, ph * HD), bf),
@@ -285,19 +306,19 @@
         pltpu.VMEM((2, n, rows, (ph + 1) * HD), bf),
         pltpu.VMEM((2, n, rows, (ph + 1) * HD), bf),
         pltpu.VMEM((2, S, LANES), jnp.float32),
-        pltpu.VMEM((T, S, width), bf),
-        pltpu.VMEM((T, S, width), bf),
-        pltpu.VMEM((T, S, width), bf),
-        pltpu.VMEM((T, S, width), bf),
+        pltpu.VMEM((2, T, S, width // 2), bf),
+        pltpu.VMEM((2, T, S, width // 2), bf),
+        pltpu.VMEM((2, T, S, width // 2), bf),
+        pltpu.VMEM((2, T, S, width // 2), bf),
         pltpu.VMEM((S, ph * HD), bf),
         dma((3,)),
         dma((2, S)),
         dma((n,)),
         dma((T,)), dma((T,)), dma((T,)), dma((T,)),
         dma((2, n)), dma((2, n)),
-        dma((T,)), dma((T,)),
-        dma((T,)), dma((T,)),
-        dma((T,)), dma((T,)), dma((T,)), dma((T,)),
+        dma((2, T)), dma((2, T)),
+        dma((2, T)), dma((2, T)),
+        dma((2, T)), dma((2, T)), dma((2, T)), dma((2, T)),
     ]
     part, full = pl.pallas_call(
         functools.partial(kernel, T, K, kvh),

time: 43.8 us -> 46.1 us (1.053)
  Pallas kernels: 43 us -> 45.3 us
    pallas_call x1, Pallas kernels: 41.8 us -> 44.1 us  [on_device(): pl.pallas_call(functools.partial(kernel, T, K, kvh), out_shape=(VOUT((S,...]
where the time goes in v3:
time: 46.1 us; the launch traced here: 46 us
  Pallas kernels  45.3 us (98%)
  between operations  0.66 us (1%)
    pallas_call x1, Pallas kernels, on_device(): pl.pallas_call(functools.partial(kernel, T, K, kvh), out_shape=(VOUT((S,...  44.1 us
    pallas_call x1, Pallas kernels, on_device(): pl.pallas_call(norm_kernel, out_shape=(jax.ShapeDtypeStruct((S, width), b...  1.17 us

profile of v3, /device:TPU:0, one launch (start us, length us, event | category | flops | bytes accessed | tf_op | source)
XLA Modules:
  0.0 46.0 jit_solution(11564323608087731105)
XLA Ops:
  0.6 0.0 copy-start
  0.6 44.1 %shard_map.86 = (bf16[16,2048]{1,0:T(8,128)(2,1)S(1)}, bf16[8,16,2048]{2,1,0:T(8,128)(2,1)S(1)}) custom-call(s32[16]{0:T(128)} %lens_ref.1, bf16[16,1024]{1,0:T(8,128)(2,1)} %q_hbm.1, bf16[2,16,4,128]{3,2,1,0:T(4,128)(2,1)} %pair_hbm.1, bf16[2,16,1024,128]{3,2,1,0:T(8,128)(2,1)} %bitcast.1, bf16[1024,16384]{1,0:T(8,128)(2,1)} %w_hbm.1, bf16[16,2048]{1,0:T(8,128)(2,1)} %res_hbm.1), custom_call_target="tpu_custom_call" | custom-call | tf_op jit(solution)/shard_map/pallas_call | solution.py:323
  44.8 0.0 copy-done
  44.8 1.2 %shard_map.87 = (bf16[16,2048]{1,0:T(8,128)(2,1)}, bf16[16,16384]{1,0:T(8,128)(2,1)}) custom-call(bf16[16,2048]{1,0:T(8,128)(2,1)S(1)} %get-tuple-element.4.part_ref, bf16[8,16,2048]{2,1,0:T(8,128)(2,1)S(1)} %get-tuple-element.5.full_ref, bf16[16384]{0:T(1024)(128)(2,1)S(1)} %copy-done), custom_call_target="tpu_custom_call" | custom-call | tf_op jit(solution)/shard_map/pallas_call | solution.py:333
Async XLA Ops:
  0.6 44.2 %copy-start = (bf16[16384]{0:T(1024)(128)(2,1)S(1)}, bf16[16384]{0:T(1024)(128)(2,1)}, u32[]{:S(2)}) copy-start(bf16[16384]{0:T(1024)(128)(2,1)} %gain_ref.1) | copy-start | bytes 98308
